TPU v7x, 32 devices: a whole 2x2x4 slice. The times are simulated.
32 devices in a mesh: grp: 2 (over x), src: 8 (over z, y), tgt: 2 (over core).
Axes of the slice: x: 2, y: 2, z: 4, core: 2. Of those that a mesh axis runs over, the one named last changes fastest.
Arguments:
- densities: bfloat16 [512, 32768], P('grp', ('src', 'tgt')), parts along dimension 0, may hold values from -6 to 6
- compress: bfloat16 [65536, 2, 256], P(('grp', 'src', 'tgt')), parts along dimension 0, may hold values from -0.0625 to 0.0625
- level_a: bfloat16 [6, 2048, 2, 256], P('grp', 'src', None, 'tgt'), parts along dimension 0, may hold values from -0.1875 to 0.1875
- level_b: bfloat16 [6, 2048, 2, 256], P('grp', 'src', None, 'tgt'), parts along dimension 0, may hold values from -0.1875 to 0.1875
- expand: bfloat16 [4096, 2, 4096], P(('grp', 'src'), None, 'tgt'), parts along dimension 0, may hold values from -0.25 to 0.25
- near_tiles: bfloat16 [2048, 128, 2, 128], P(('grp', 'src', 'tgt')), parts along dimension 0, may hold values from -0.375 to 0.375
- tile_pairs: int32 [2048, 2], P(('grp', 'src', 'tgt')), parts along dimension 0, may hold values from 0 to 15
- tile_count: int32 [32], P(('grp', 'src', 'tgt')), parts along dimension 0, may hold values from 1 to 63, as said below
- cluster_order: int32 [32, 16], P(('grp', 'src', 'tgt')), parts along dimension 0, may hold values from 0 to 15, each once within a row
Outputs:
- potential: bfloat16 [512, 32768], P('grp', ('src', 'tgt')), parts along dimension 0
There are 2 independent parts, one for each index of `grp`. A program takes and returns all parts, laid end to end along the dimension named above; each array names one. Nothing has to cross between parts.
Inputs may be any that keep to these rules, and one draw needn't show every extreme that they name: For every i below 8, tile_count[i] + tile_count[i + 8] == 64; slots at or beyond a device's count are unused. `cluster_order`: each row is a permutation.
All inputs are finite; a program needn't handle non-finite values.
Results may differ from a plain program's by a relative error of at most 0.007.
Values may be sent and summed in bfloat16 or wider, within the bound.
A program may use at most 128 MiB of HBM per device.

v0:
```python
import jax
import jax.numpy as jnp
from jax import lax
from jax.sharding import PartitionSpec as P


def swapped(value, axis, bit):
    mask = 2**bit
    pairs = [(source, source ^ mask) for source in range(lax.axis_size(axis))]
    return lax.ppermute(value, axis, pairs)


def complex_product(operand, matrix):
    product = jnp.dot(operand, matrix, preferred_element_type=jnp.float32)
    half_rows = operand.shape[0] // 2
    half_cols = matrix.shape[1] // 2
    real_part = product[:half_rows, :half_cols] - product[half_rows:, half_cols:]
    imag_part = product[:half_rows, half_cols:] + product[half_rows:, :half_cols]
    return jnp.concatenate([real_part, imag_part], axis=0)


def near_sum(sources, tile_blocks, source_ids, target_ids, active, targets):
    half_rows = sources.shape[0] // 2
    cluster_size = tile_blocks.shape[1]
    picked = jnp.take(sources, source_ids, axis=1)
    product = jnp.einsum("rjp,jpq->rjq", picked, tile_blocks, preferred_element_type=jnp.float32)
    real_part = product[:half_rows, :, :cluster_size] - product[half_rows:, :, cluster_size:]
    imag_part = product[:half_rows, :, cluster_size:] + product[half_rows:, :, :cluster_size]
    joined = jnp.concatenate([real_part, imag_part], axis=0)
    chooser = (
        (target_ids[:, None] == jnp.arange(targets, dtype=jnp.int32)[None, :]) & active[:, None]
    ).astype(jnp.float32)
    return jnp.einsum("rjq,jc->rcq", joined, chooser, precision=lax.Precision.HIGHEST)


def shards(
    densities, compress, level_a, level_b, expand, near_tiles, tile_pairs, tile_count, cluster_order
):
    row_count, points = densities.shape
    rank = compress.shape[2]
    sections = level_a.shape[0]
    partial_value = complex_product(densities, compress.reshape(points, 2 * rank))
    matrices_a = level_a.reshape(sections, rank, -1)
    matrices_b = level_b.reshape(sections, rank, -1)
    coefficients = lax.psum(partial_value, "tgt").astype(jnp.bfloat16)
    for section in range(sections):
        partner_coeff = swapped(coefficients, "src", section)
        updated = complex_product(coefficients, matrices_a[section]) + complex_product(
            partner_coeff, matrices_b[section]
        )
        coefficients = lax.all_gather(updated.astype(jnp.bfloat16), "tgt", axis=1, tiled=True)
    far_field = complex_product(coefficients, expand.reshape(rank, 2 * points))
    clusters = cluster_order.shape[1]
    cluster_size = points // clusters
    placed = (
        jnp.zeros((row_count, clusters, cluster_size), jnp.float32)
        .at[:, cluster_order[0], :]
        .set(far_field.reshape(row_count, clusters, cluster_size))
    )
    slots = near_tiles.shape[0]
    blocks = near_tiles.reshape(slots, cluster_size, 2 * cluster_size)
    sources = densities.reshape(row_count, clusters, cluster_size)
    count = tile_count[0]
    active = jnp.arange(slots, dtype=jnp.int32) < count
    near_field = near_sum(sources, blocks, tile_pairs[:, 1], tile_pairs[:, 0], active, clusters)
    return (placed + near_field).reshape(row_count, points).astype(jnp.bfloat16)


def solution(mesh):
    placed = (
        P("grp", ("src", "tgt")),
        P(("grp", "src", "tgt"), None, None),
        P("grp", "src", None, "tgt"),
        P("grp", "src", None, "tgt"),
        P(("grp", "src"), None, "tgt"),
        P(("grp", "src", "tgt"), None, None, None),
        P(("grp", "src", "tgt"), None),
        P(("grp", "src", "tgt")),
        P(("grp", "src", "tgt"), None),
    )
    return jax.shard_map(
        shards, mesh=mesh, in_specs=placed, out_specs=P("grp", ("src", "tgt")), check_vma=False
    )
```

profile of v0, /device:TPU:0, one launch (start us, length us, event | category | flops | bytes accessed | tf_op | source)
XLA Modules:
  0.0 93.4 jit_solution(9930778493908321840)
XLA Ops:
  0.0 2.1 %copy.22 = bf16[256,8,2,256]{3,1,2,0:T(8,128)(2,1)S(1)} copy(bf16[256,8,2,256]{3,2,1,0:T(2,128)(2,1)} %bitcast.84) | data formatting | bytes 4194304
  2.2 0.7 fusion.40
  2.9 4.5 %all-reduce.1 = bf16[256,256]{1,0:T(8,128)(2,1)S(1)} all-reduce(f32[256,256]{1,0:T(8,128)S(1)} %pad_maximum_fusion.1), channel_id=1, replica_groups=mesh['grp'=2,'src'=8,'tgt'=2] {'tgt'}, use_global_device_ids=true, to_apply=%region_0.0 | all-reduce | flops 65536 | bytes 393216 | tf_op jit(solution)/shard_map/psum | solution.py:45
  7.5 2.7 %collective-permute-start = (bf16[256,256]{1,0:T(8,128)(2,1)S(1)}, bf16[256,256]{1,0:T(8,128)(2,1)S(1)}, u32[]{:S(2)}, u32[]{:S(2)}) collective-permute-start(bf16[256,256]{1,0:T(8,128)(2,1)S(1)} %all-reduce.1), channel_id=1, source_target_pairs={{0,2},{2,0},{4,6},{6,4},{8,10},{10,8},{12,14},{14,12},{1,3},{3,1},... | collective-permute-start | bytes 393224 | tf_op jit(solution)/shard_map/ppermute | solution.py:10
  10.2 0.5 copy.17
  10.7 0.3 fusion.38
  11.0 1.3 %fusion.39 = (bf16[1,256,2,128]{3,2,1,0:T(2,128)(2,1)S(1)}, bf16[1,256,2,128]{3,2,1,0:T(2,128)(2,1)S(1)}, bf16[1,256,2,128]{3,2,1,0:T(2,128)(2,1)S(1)}) fusion(bf16[3,256,2,128]{3,2,1,0:T(2,128)(2,1)} %param.11), kind=kLoop, calls=%fused_computation.73 | loop fusion | bytes 786432 | tf_op jit(solution)/shard_map/slice | solution.py:48
  12.3 0.2 fusion.24
  12.6 0.7 copy.18
  13.2 7.6 %reshape.71 = bf16[64,128,256]{2,1,0:T(8,128)(2,1)} reshape(bf16[64,128,2,128]{3,2,1,0:T(2,128)(2,1)} %param.14) | data formatting | bytes 8388608 | tf_op jit(solution)/shard_map/reshape | solution.py:61
  20.8 3.0 %gather_fusion = bf16[64,256,128]{2,1,0:T(8,128)(2,1)} fusion(bf16[256,16,128]{2,0,1:T(8,128)(2,1)S(1)} %copy.18, s32[1024]{0:T(1024)S(1)} %pad_clamp_fusion), kind=kCustom, calls=%fused_computation | custom fusion | bytes 8388864 | tf_op jit(solution)/shard_map/jit(_take)/gather | solution.py:25
  23.9 11.6 %convolution_bitcast_fusion = f32[256,64,256]{2,0,1:T(8,128)} fusion(bf16[64,128,256]{2,1,0:T(8,128)(2,1)} %reshape.71, bf16[64,256,128]{2,1,0:T(8,128)(2,1)} %gather_fusion, pred[64]{0:T(512)(128)(4,1)S(1)} %and_bitcast_fusion), kind=kOutput, calls=%fused_computation.2 | convolution fusion | flops 1075838976 | bytes 25165888 | tf_op jit(solution)/shard_map/rjp,jpq->rjq/dot_general | solution.py:26
  35.5 10.1 %slice_subtract_fusion = (f32[128,64,128]{2,0,1:T(8,128)S(1)}, f32[128,64,128]{2,0,1:T(8,128)}) fusion(f32[256,64,256]{2,0,1:T(8,128)} %convolution_bitcast_fusion), kind=kLoop, calls=%fused_computation.7 | loop fusion | flops 2097152 | bytes 25165824 | tf_op jit(solution)/shard_map/sub | solution.py:27
  45.6 6.3 %pad_maximum_fusion = f32[256,64,128]{2,0,1:T(8,128)} fusion(f32[128,64,128]{2,0,1:T(8,128)} %get-tuple-element.6, f32[128,64,128]{2,0,1:T(8,128)S(1)} %get-tuple-element.5), kind=kLoop, calls=%fused_computation.3 | loop fusion | flops 2097152 | bytes 16777216 | tf_op jit(solution)/shard_map/concatenate | solution.py:29
  51.9 0.9 copy.29
  53.5 0.2 fusion.21
  53.8 1.9 %all_gather.9 = bf16[256,256]{1,0:T(8,128)(2,1)S(1)} all-gather(bf16[256,128]{1,0:T(8,128)(2,1)S(1)} %fusion.27), channel_id=1, replica_groups=mesh['grp'=2,'src'=8,'tgt'=2] {'tgt'}, dimensions={1}, use_global_device_ids=true | all-gather | bytes 196608 | tf_op jit(solution)/shard_map/all_gather | solution.py:51
  55.7 1.6 %collective-permute-start.1 = (bf16[256,256]{1,0:T(8,128)(2,1)S(1)}, bf16[256,256]{1,0:T(8,128)(2,1)S(1)}, u32[]{:S(2)}, u32[]{:S(2)}) collective-permute-start(bf16[256,256]{1,0:T(8,128)(2,1)S(1)} %all_gather.9), channel_id=1, source_target_pairs={{0,4},{2,6},{4,0},{6,2},{8,12},{10,14},{12,8},{14,10},{1,5},{3,7},... | collective-permute-start | bytes 393224 | tf_op jit(solution)/shard_map/ppermute | solution.py:10
  57.5 3.8 %collective-permute-done.1 = bf16[256,256]{1,0:T(8,128)(2,1)S(1)} collective-permute-done((bf16[256,256]{1,0:T(8,128)(2,1)S(1)}, bf16[256,256]{1,0:T(8,128)(2,1)S(1)}, u32[]{:S(2)}, u32[]{:S(2)}) %collective-permute-start.1) | collective-permute-done | bytes 131104 | tf_op jit(solution)/shard_map/ppermute | solution.py:10
  61.2 0.2 fusion.15
  61.5 1.9 %all_gather.10 = bf16[256,256]{1,0:T(8,128)(2,1)S(1)} all-gather(bf16[256,128]{1,0:T(8,128)(2,1)S(1)} %fusion.28), channel_id=1, replica_groups=mesh['grp'=2,'src'=8,'tgt'=2] {'tgt'}, dimensions={1}, use_global_device_ids=true | all-gather | bytes 196608 | tf_op jit(solution)/shard_map/all_gather | solution.py:51
  63.4 2.6 %collective-permute-start.2 = (bf16[256,256]{1,0:T(8,128)(2,1)S(1)}, bf16[256,256]{1,0:T(8,128)(2,1)S(1)}, u32[]{:S(2)}, u32[]{:S(2)}) collective-permute-start(bf16[256,256]{1,0:T(8,128)(2,1)S(1)} %all_gather.10), channel_id=1, source_target_pairs={{0,8},{2,10},{4,12},{6,14},{8,0},{10,2},{12,4},{14,6},{1,9},{3,11}... | collective-permute-start | bytes 393224 | tf_op jit(solution)/shard_map/ppermute | solution.py:10
  66.2 6.5 %collective-permute-done.2 = bf16[256,256]{1,0:T(8,128)(2,1)S(1)} collective-permute-done((bf16[256,256]{1,0:T(8,128)(2,1)S(1)}, bf16[256,256]{1,0:T(8,128)(2,1)S(1)}, u32[]{:S(2)}, u32[]{:S(2)}) %collective-permute-start.2) | collective-permute-done | bytes 131104 | tf_op jit(solution)/shard_map/ppermute | solution.py:10
  72.7 0.2 fusion.9
  72.9 2.1 %all_gather.11 = bf16[256,256]{1,0:T(8,128)(2,1)S(1)} all-gather(bf16[256,128]{1,0:T(8,128)(2,1)S(1)} %fusion.29), channel_id=1, replica_groups=mesh['grp'=2,'src'=8,'tgt'=2] {'tgt'}, dimensions={1}, use_global_device_ids=true | all-gather | bytes 196608 | tf_op jit(solution)/shard_map/all_gather | solution.py:51
  75.0 0.7 fusion.41
  75.8 0.3 slice_subtract_fusion.1
  76.1 1.6 %bitcast_bitcast_fusion = f32[16,256,128]{2,1,0:T(8,128)} fusion(f32[128,2048]{1,0:T(8,128)S(1)} %get-tuple-element.8, f32[128,2048]{1,0:T(8,128)S(1)} %get-tuple-element.7), kind=kLoop, calls=%fused_computation.11 | loop fusion | flops 524288 | bytes 4194304 | tf_op jit(solution)/shard_map/reshape | solution.py:58
  77.7 0.2 broadcast_in_dim.16
  77.9 2.7 %scatter_fusion = f32[256,16,128]{2,0,1:T(8,128)S(1)} fusion(f32[256,16,128]{2,0,1:T(8,128)S(1)} %broadcast_in_dim.16, s32[16]{0:T(128)S(1)} %fusion.35, f32[16,256,128]{2,1,0:T(8,128)} %bitcast_bitcast_fusion), kind=kCustom, calls=%fused_computation.1 | custom fusion | bytes 6291520 | tf_op jit(solution)/shard_map/scatter | solution.py:58
  80.6 11.6 %fusion.5 = bf16[256,16,128]{2,1,0:T(8,128)(2,1)S(1)} fusion(f32[256,16,128]{2,0,1:T(8,128)S(1)} %scatter_fusion, f32[256,64,128]{2,0,1:T(8,128)} %pad_maximum_fusion, s32[64]{0:T(128)S(1)} %get-tuple-element.29, pred[64]{0:T(512)(128)(4,1)S(1)} %iota_compare_fusion.1), kind=kOutput, calls=%fused_computation.14 | convolution fusion | flops 403703808 | bytes 11534656 | tf_op jit(solution)/shard_map/rjq,jc->rcq/dot_general | solution.py:33
  92.2 1.2 %copy.62 = bf16[32,8,16,128]{3,1,2,0:T(8,128)(2,1)} copy(bf16[32,8,16,128]{3,2,1,0:T(8,128)(2,1)S(1)} %bitcast.82) | data formatting | bytes 2097152
  (29 shorter events, 0.6 us)
Async XLA Ops:
  0.0 2.2 %copy-start.1 = (bf16[256,2048]{1,0:T(8,128)(2,1)S(1)}, bf16[256,2048]{1,0:T(8,128)(2,1)}, u32[]{:S(2)}) copy-start(bf16[256,2048]{1,0:T(8,128)(2,1)} %param.9) | copy-start | bytes 3145732
  2.1 8.6 %copy-start.3 = (s32[64,2]{0,1:T(2,128)S(1)}, s32[64,2]{0,1:T(2,128)}, u32[]{:S(2)}) copy-start(s32[64,2]{0,1:T(2,128)} %param.15) | copy-start | bytes 1540
  2.1 8.6 %copy-start.2 = (bf16[3,256,2,128]{3,2,1,0:T(2,128)(2,1)S(1)}, bf16[3,256,2,128]{3,2,1,0:T(2,128)(2,1)}, u32[]{:S(2)}) copy-start(bf16[3,256,2,128]{3,2,1,0:T(2,128)(2,1)} %param.12) | copy-start | bytes 1179652
  7.5 46.0 %collective-permute-start = (bf16[256,256]{1,0:T(8,128)(2,1)S(1)}, bf16[256,256]{1,0:T(8,128)(2,1)S(1)}, u32[]{:S(2)}, u32[]{:S(2)}) collective-permute-start(bf16[256,256]{1,0:T(8,128)(2,1)S(1)} %all-reduce.1), channel_id=1, source_target_pairs={{0,2},{2,0},{4,6},{6,4},{8,10},{10,8},{12,14},{14,12},{1,3},{3,1},... | collective-permute-start | bytes 393224 | tf_op jit(solution)/shard_map/ppermute | solution.py:10
  45.6 6.3 %copy-start.4 = (s32[1,16]{1,0:T(1,128)S(1)}, s32[1,16]{1,0:T(1,128)}, u32[]{:S(2)}) copy-start(s32[1,16]{1,0:T(1,128)} %param.17) | copy-start | bytes 196
  45.6 6.3 %copy-start = (bf16[256,2,2048]{2,1,0:T(2,128)(2,1)S(1)}, bf16[256,2,2048]{2,1,0:T(2,128)(2,1)}, u32[]{:S(2)}) copy-start(bf16[256,2,2048]{2,1,0:T(2,128)(2,1)} %param.13) | copy-start | bytes 6291460
  55.7 5.6 %collective-permute-start.1 = (bf16[256,256]{1,0:T(8,128)(2,1)S(1)}, bf16[256,256]{1,0:T(8,128)(2,1)S(1)}, u32[]{:S(2)}, u32[]{:S(2)}) collective-permute-start(bf16[256,256]{1,0:T(8,128)(2,1)S(1)} %all_gather.9), channel_id=1, source_target_pairs={{0,4},{2,6},{4,0},{6,2},{8,12},{10,14},{12,8},{14,10},{1,5},{3,7},... | collective-permute-start | bytes 393224 | tf_op jit(solution)/shard_map/ppermute | solution.py:10
  63.4 9.3 %collective-permute-start.2 = (bf16[256,256]{1,0:T(8,128)(2,1)S(1)}, bf16[256,256]{1,0:T(8,128)(2,1)S(1)}, u32[]{:S(2)}, u32[]{:S(2)}) collective-permute-start(bf16[256,256]{1,0:T(8,128)(2,1)S(1)} %all_gather.10), channel_id=1, source_target_pairs={{0,8},{2,10},{4,12},{6,14},{8,0},{10,2},{12,4},{14,6},{1,9},{3,11}... | collective-permute-start | bytes 393224 | tf_op jit(solution)/shard_map/ppermute | solution.py:10
where the time goes:
time: 93.8 us; the launch traced here: 93.4 us
  matrix products  25.7 us (27%)
  local copies, waits for them, and re-layouts  20.6 us (22%)
  other arithmetic  18.6 us (20%)
  blocking collectives  10.5 us (11%)
  waiting for transfers between devices  10.2 us (11%)
  starting transfers between devices  6.88 us (7%)
  between operations  0.95 us (1%)
    dot_general x1, matrix products, near_sum(): jnp.einsum('rjp,jpq->rjq', picked, tile_blocks, preferred_element_type=jn...  11.6 us
    dot_general x1, matrix products, near_sum(): jnp.einsum('rjq,jc->rcq', joined, chooser, precision=lax.Precision.HIGHEST)  11.6 us
    ppermute x3, waiting for transfers between devices, swapped(): return lax.ppermute(value, axis, pairs)  10.2 us
    sub x1, other arithmetic, near_sum(): product[:half_rows, :, :cluster_size]  10.1 us
    reshape x1, local copies, waits for them, and re-layouts, shards(): blocks = near_tiles.reshape(slots, cluster_size, 2 * cluster_size)  7.59 us
    ppermute x3, starting transfers between devices, swapped(): return lax.ppermute(value, axis, pairs)  6.88 us
    concatenate x1, other arithmetic, near_sum(): joined = jnp.concatenate([real_part, imag_part], axis=0)  6.32 us
    all_gather x3, blocking collectives, shards(): lax.all_gather(updated.astype(jnp.bfloat16), 'tgt', axis=1, tiled=True)  5.97 us
  transfers between devices with their start and end apart: 3, of which 2 were waited for; matrix products, arithmetic and copies ran while one was open for 46% of the time, Pallas kernels for 0%

commit v1 on v0

v1 whole, which is shorter than its diff:
```python
import functools

import jax
import jax.numpy as jnp
from jax import lax
from jax.experimental import pallas as pl
from jax.experimental.pallas import tpu as pltpu
from jax.sharding import PartitionSpec as P

MESH = pl.DeviceIdType.MESH
CHUNKS = 2
UNROLL = 4


def lift(real, imag, perm):
    upper = jnp.concatenate([real, -imag], axis=1)
    lower = jnp.concatenate([imag, real], axis=1)
    both = jnp.concatenate([upper, lower], axis=0)
    return jnp.dot(both, perm, preferred_element_type=jnp.float32).astype(jnp.bfloat16)


def flat(block):
    return block.reshape(block.shape[0] * 2, block.shape[2])


def kernel(
    sizes,
    dens_h, comp_h, la_h, lb_h, exp_h, tiles_h, pairs_s, count_s, order_s,
    out_h,
    dens_v, comp_v, lev_v, exp_v, tiles_v, lifted_v, sums_v, part_v, part_r, coef_v, recv_v, fin_v, out_v,
    dens_sem, comp_sem, lev_sem, levs_sem, levr_sem, exp_sem, tiles_sem, part_sem, send_sem, recv_sem, fin_sem, out_sem,
):
    levels, clusters, width, slots, rhs, rank, n_tgt = sizes
    src, tgt = lax.axis_index("src"), lax.axis_index("tgt")
    other = 1 - tgt
    sibling = {"tgt": other}
    partners = [{"src": src ^ (1 << level)} for level in range(levels)]
    lanes = rank // width
    comp_parts = comp_sem.shape[1]
    rows_part = comp_h.shape[0] // comp_parts
    tile_parts = tiles_sem.shape[0]
    slots_part = slots // tile_parts

    loads_dens = pltpu.make_async_copy(dens_h, dens_v, dens_sem)
    loads_dens.start()
    loads_comp = [
        [
            pltpu.make_async_copy(
                comp_h.at[pl.ds(part * rows_part, rows_part), :, pl.ds(lane * width, width)],
                comp_v.at[lane, pl.ds(part * rows_part, rows_part)],
                comp_sem.at[lane, part],
            )
            for lane in range(lanes)
        ]
        for part in range(comp_parts)
    ]
    for part in loads_comp:
        for item in part:
            item.start()
    barrier = pltpu.get_barrier_semaphore()
    for target in [sibling] + partners:
        pl.semaphore_signal(barrier, inc=1, device_id=target, device_id_type=MESH)
    factors = (la_h, lb_h)
    loads_lev = [pltpu.make_async_copy(factors[ab], lev_v.at[ab, tgt], lev_sem.at[ab]) for ab in range(2)]
    for item in loads_lev:
        item.start()
    loads_tiles = [
        pltpu.make_async_copy(
            tiles_h.at[pl.ds(part * slots_part, slots_part)],
            tiles_v.at[pl.ds(part * slots_part, slots_part)],
            tiles_sem.at[part],
        )
        for part in range(tile_parts)
    ]
    for item in loads_tiles:
        item.start()
    loads_exp = [
        pltpu.make_async_copy(exp_h.at[:, :, pl.ds(c * width, width)], exp_v.at[c], exp_sem.at[c])
        for c in range(clusters)
    ]
    for item in loads_exp:
        item.start()

    row = lax.broadcasted_iota(jnp.int32, (2 * width, 2 * width), 0)
    col = lax.broadcasted_iota(jnp.int32, (2 * width, 2 * width), 1)
    spot = jnp.where(row < width, 2 * row, 2 * (row - width) + 1)
    perm = (spot == col).astype(jnp.float32).astype(jnp.bfloat16)

    pl.semaphore_wait(barrier, 1 + levels)
    swaps_lev = [
        pltpu.make_async_remote_copy(
            src_ref=factors[ab], dst_ref=lev_v.at[ab, tgt], send_sem=levs_sem.at[ab], recv_sem=levr_sem.at[ab],
            device_id=sibling, device_id_type=MESH,
        )
        for ab in range(2)
    ]
    for item in swaps_lev:
        item.start()

    loads_dens.wait()
    for c in range(clusters):
        cut = pl.ds(c * width, width)
        lifted_v[c] = lift(dens_v[:rhs, cut], dens_v[rhs:, cut], perm)
    per_part = clusters // comp_parts
    sums = [jnp.zeros((2 * rhs, width), jnp.float32) for _ in range(lanes)]
    for part in range(comp_parts):
        for item in loads_comp[part]:
            item.wait()
        for c in range(part * per_part, (part + 1) * per_part):
            block = lifted_v[c]
            for lane in range(lanes):
                sums[lane] = sums[lane] + jnp.dot(
                    block, flat(comp_v[lane, pl.ds(c * width, width)]), preferred_element_type=jnp.float32
                )
    half = rhs // n_tgt
    for h in range(n_tgt):
        for ri in range(2):
            for lane in range(lanes):
                part_v[h, ri, :, pl.ds(lane * width, width)] = sums[lane][ri * rhs + h * half : ri * rhs + (h + 1) * half]
    swap_part = pltpu.make_async_remote_copy(
        src_ref=part_v.at[other], dst_ref=part_r, send_sem=part_sem.at[0], recv_sem=part_sem.at[1],
        device_id=sibling, device_id_type=MESH,
    )
    swap_part.start()

    rows = half // CHUNKS

    def send(level, q):
        copy = pltpu.make_async_remote_copy(
            src_ref=coef_v.at[level, q], dst_ref=recv_v.at[level, q],
            send_sem=send_sem.at[level, q], recv_sem=recv_sem.at[level, q],
            device_id=partners[level], device_id_type=MESH,
        )
        copy.start()
        return copy

    def lifted(value):
        return jnp.concatenate(
            [
                lift(value[0, :, lane * width : (lane + 1) * width], value[1, :, lane * width : (lane + 1) * width], perm)
                for lane in range(lanes)
            ],
            axis=1,
        )

    def apply(value, ab, level):
        return jnp.concatenate(
            [
                jnp.dot(value, flat(lev_v[ab, h, level]), preferred_element_type=jnp.float32)
                for h in range(n_tgt)
            ],
            axis=1,
        )

    count = count_s[0]
    last = [jnp.int32(slots) for _ in range(clusters)]
    sums_v[slots] = jnp.zeros((2 * rhs, width), jnp.float32)

    def near_step(step, last):
        last = list(last)
        base = step * UNROLL
        terms = [
            jnp.dot(lifted_v[pairs_s[1, base + u]], flat(tiles_v[base + u]), preferred_element_type=jnp.float32)
            for u in range(UNROLL)
        ]
        for u in range(UNROLL):
            slot = base + u
            target = pairs_s[0, slot]
            active = slot < count
            before = jnp.int32(slots)
            for c in range(clusters):
                hit = target == c
                before = jnp.where(hit, last[c], before)
                last[c] = jnp.where(hit & active, slot, last[c])
            sums_v[slot] = terms[u] + sums_v[before]
        return tuple(last)

    swap_part.wait()
    sends = []
    for q in range(CHUNKS):
        cut = pl.ds(q * rows, rows)
        coef_v[0, q] = (part_v[tgt, :, cut, :] + part_r[:, cut, :]).astype(jnp.bfloat16)
        sends.append(send(0, q))
    for item in loads_lev:
        item.wait()
    for item in swaps_lev:
        item.wait()
    current = sends
    done_sends = []
    swaps_fin = []
    tiles_waited = 0
    for level in range(levels):
        own = [apply(lifted(coef_v[level, q]), 0, level) for q in range(CHUNKS)]
        first, final = (tile_parts * level) // levels, (tile_parts * (level + 1)) // levels
        for part in range(first, final):
            loads_tiles[part].wait()
        last = lax.fori_loop(
            first * slots_part // UNROLL, final * slots_part // UNROLL, near_step, tuple(last)
        )
        following = []
        for q in range(CHUNKS):
            current[q].wait_recv()
            total = own[q] + apply(lifted(recv_v[level, q]), 1, level)
            fresh = jnp.stack([total[:rows], total[rows:]]).astype(jnp.bfloat16)
            if level + 1 < levels:
                coef_v[level + 1, q] = fresh
                following.append(send(level + 1, q))
            else:
                fin_v[tgt, q] = fresh
                copy = pltpu.make_async_remote_copy(
                    src_ref=fin_v.at[tgt, q], dst_ref=fin_v.at[tgt, q],
                    send_sem=fin_sem.at[0, q], recv_sem=fin_sem.at[1, q],
                    device_id=sibling, device_id_type=MESH,
                )
                copy.start()
                swaps_fin.append(copy)
        done_sends += current
        current = following
    for item in loads_exp:
        item.wait()
    for item in swaps_fin:
        item.wait()
    for item in done_sends:
        item.wait_send()

    whole = [
        jnp.concatenate([fin_v[h, q, ri] for h in range(n_tgt) for q in range(CHUNKS)], axis=0) for ri in range(2)
    ]
    operand = jnp.concatenate(
        [
            lift(whole[0][:, lane * width : (lane + 1) * width], whole[1][:, lane * width : (lane + 1) * width], perm)
            for lane in range(lanes)
        ],
        axis=1,
    )
    out_parts = out_sem.shape[0]
    per_out = clusters // out_parts
    stores = []
    for part in range(out_parts):
        for t in range(part * per_out, (part + 1) * per_out):
            origin = jnp.int32(0)
            for c in range(clusters):
                origin = jnp.where(order_s[0, c] == t, c, origin)
            far = jnp.dot(operand, flat(exp_v[origin]), preferred_element_type=jnp.float32)
            out_v[:, pl.ds(t * width, width)] = (far + sums_v[last[t]]).astype(jnp.bfloat16)
        cut = pl.ds(part * per_out * width, per_out * width)
        stores.append(pltpu.make_async_copy(out_v.at[:, cut], out_h.at[:, cut], out_sem.at[part]))
        stores[-1].start()
    for item in stores:
        item.wait()


def shards(
    densities, compress, level_a, level_b, expand, near_tiles, tile_pairs, tile_count, cluster_order
):
    row_count, points = densities.shape
    rhs = row_count // 2
    rank = compress.shape[2]
    levels = level_a.shape[0]
    clusters = cluster_order.shape[1]
    width = points // clusters
    slots = near_tiles.shape[0]
    n_tgt = lax.axis_size("tgt")
    sizes = (levels, clusters, width, slots, rhs, rank, n_tgt)
    lanes = rank // width
    rows = rhs // n_tgt // CHUNKS
    comp_parts, tile_parts, out_parts = 4, 16, 4
    bf16, f32 = jnp.bfloat16, jnp.float32
    anywhere = pl.BlockSpec(memory_space=pl.ANY)
    scalar = pl.BlockSpec(memory_space=pltpu.SMEM)
    dma = pltpu.SemaphoreType.DMA
    return pl.pallas_call(
        functools.partial(kernel, sizes),
        out_shape=jax.ShapeDtypeStruct((row_count, points), bf16),
        in_specs=[anywhere] * 6 + [scalar] * 3,
        out_specs=anywhere,
        scratch_shapes=[
            pltpu.VMEM((row_count, points), bf16),
            pltpu.VMEM((lanes, points, 2, width), bf16),
            pltpu.VMEM((2, n_tgt, levels, rank, 2, width), bf16),
            pltpu.VMEM((clusters, rank, 2, width), bf16),
            pltpu.VMEM((slots, width, 2, width), bf16),
            pltpu.VMEM((clusters, row_count, 2 * width), bf16),
            pltpu.VMEM((slots + 1, row_count, width), f32),
            pltpu.VMEM((n_tgt, 2, rhs // n_tgt, rank), f32),
            pltpu.VMEM((2, rhs // n_tgt, rank), f32),
            pltpu.VMEM((levels, CHUNKS, 2, rows, rank), bf16),
            pltpu.VMEM((levels, CHUNKS, 2, rows, rank), bf16),
            pltpu.VMEM((n_tgt, CHUNKS, 2, rows, rank), bf16),
            pltpu.VMEM((row_count, points), bf16),
            dma,
            dma((lanes, comp_parts)),
            dma((2,)),
            dma((2,)),
            dma((2,)),
            dma((clusters,)),
            dma((tile_parts,)),
            dma((2,)),
            dma((levels, CHUNKS)),
            dma((levels, CHUNKS)),
            dma((2, CHUNKS)),
            dma((out_parts,)),
        ],
        compiler_params=pltpu.CompilerParams(collective_id=0, has_side_effects=True),
    )(densities, compress, level_a, level_b, expand, near_tiles, tile_pairs.T, tile_count, cluster_order)


def solution(mesh):
    placed = (
        P("grp", ("src", "tgt")),
        P(("grp", "src", "tgt"), None, None),
        P("grp", "src", None, "tgt"),
        P("grp", "src", None, "tgt"),
        P(("grp", "src"), None, "tgt"),
        P(("grp", "src", "tgt"), None, None, None),
        P(("grp", "src", "tgt"), None),
        P(("grp", "src", "tgt")),
        P(("grp", "src", "tgt"), None),
    )
    return jax.shard_map(
        shards, mesh=mesh, in_specs=placed, out_specs=P("grp", ("src", "tgt")), check_vma=False
    )
```

time: 93.8 us -> 28.1 us (0.30)
  matrix products: 25.7 us -> 0 us
  Pallas kernels: 0 us -> 25 us
  other arithmetic: 18.6 us -> 0 us
  local copies, waits for them, and re-layouts: 20.6 us -> 2.3 us
  blocking collectives: 10.5 us -> 0 us
  waiting for transfers between devices: 10.2 us -> 0 us
  starting transfers between devices: 6.88 us -> 0 us
    dot_general x10 -> x0, matrix products: 25.7 us -> none  [the longest x1 11.6 us: near_sum(): jnp.einsum('rjp,jpq->rjq', picked, tile_blocks, preferred_element_type=jn...]
    pallas_call x0 -> x1, Pallas kernels: none -> 25 us  [shards(): pl.pallas_call(functools.partial(kernel, sizes), out_shape=jax.ShapeDtype...]
    sub x9 -> x0, other arithmetic: 10.6 us -> none  [the longest x1 10.1 us: near_sum(): product[:half_rows, :, :cluster_size]]
    ppermute x3 -> x0, waiting for transfers between devices: 10.2 us -> none  [swapped(): return lax.ppermute(value, axis, pairs)]
    reshape x2 -> x0, local copies, waits for them, and re-layouts: 8.25 us -> none  [the longest x1 7.59 us: shards(): blocks = near_tiles.reshape(slots, cluster_size, 2 * cluster_size)]
    ppermute x3 -> x0, starting transfers between devices: 6.88 us -> none  [swapped(): return lax.ppermute(value, axis, pairs)]
    concatenate x2 -> x0, other arithmetic: 6.34 us -> none  [the longest x1 6.32 us: near_sum(): joined = jnp.concatenate([real_part, imag_part], axis=0)]
    all_gather x3 -> x0, blocking collectives: 5.97 us -> none  [shards(): lax.all_gather(updated.astype(jnp.bfloat16), 'tgt', axis=1, tiled=True)]
  transfers between devices with their start and end apart: 3 -> 0, of which waited for: 2 -> 0; matrix products, arithmetic and copies ran while one was open for 46% -> 0% of each run, Pallas kernels for 0% -> 0%
where the time goes in v1:
time: 28.1 us; the launch traced here: 28 us
  Pallas kernels  25 us (89%)
  local copies, waits for them, and re-layouts  2.3 us (8%)
  between operations  0.66 us (2%)
    pallas_call x1, Pallas kernels, shards(): pl.pallas_call(functools.partial(kernel, sizes), out_shape=jax.ShapeDtype...  25 us
    unnamed x1, local copies, waits for them, and re-layouts  2.3 us

profile of v1, /device:TPU:0, one launch (start us, length us, event | category | flops | bytes accessed | tf_op | source)
XLA Modules:
  0.0 28.0 jit_solution(8164705942211654304)
XLA Ops:
  0.7 25.0 %shard_map.91 = bf16[256,2048]{1,0:T(8,128)(2,1)} custom-call(bf16[256,2048]{1,0:T(8,128)(2,1)} %dens_h.1, bf16[2048,2,256]{2,1,0:T(2,128)(2,1)} %comp_h.1, bf16[3,256,2,128]{3,2,1,0:T(2,128)(2,1)} %la_h.1, bf16[3,256,2,128]{3,2,1,0:T(2,128)(2,1)} %lb_h.1, bf16[256,2,2048]{2,1,0:T(2,128)(2,1)} %exp_h.1, bf16[64,128,2,128]{3,2,1,0:T(2,128)(2,1)} %tiles_h.1, ...), custom_call_target="tpu_custom_call" | custom-call | tf_op jit(solution)/shard_map/pallas_call | solution.py:272
  25.7 2.3 %copy.12 = bf16[256,2048]{1,0:T(8,128)(2,1)} copy(bf16[256,2048]{1,0:T(8,128)(2,1)} %shard_map.91) | data formatting | bytes 2097152
